TPU v7x, 8 devices: a whole 2x2x1 slice. The times are simulated.
8 devices in a mesh: dp: 1 (over z), sp: 8 (over y, x, core).
Axes of the slice: x: 2, y: 2, z: 1, core: 2. Of those that a mesh axis runs over, the one named last changes fastest.
Arguments:
- hidden: bfloat16 [512, 2048], P('dp')
- w_norm: bfloat16 [2048], replicated
- w_q: bfloat16 [2048, 2048], replicated
- w_k: bfloat16 [2048, 256], replicated
- w_v: bfloat16 [2048, 256], replicated
- w_o: bfloat16 [2048, 2048], replicated
- k_cache: bfloat16 [512, 1024, 256], P('dp', 'sp')
- v_cache: bfloat16 [512, 1024, 256], P('dp', 'sp')
- cache_len: int32 [512], P('dp')
Outputs:
- output 1: bfloat16 [512, 2048], P('dp')
- output 2: bfloat16 [512, 1024, 256], P('dp', 'sp')
- output 3: bfloat16 [512, 1024, 256], P('dp', 'sp')
All inputs are finite; a program needn't handle non-finite values.
Results may differ from a plain program's by a relative error of at most 0.0133847.
Values sent between devices are 32-bit elements.
A program may use at most 1 GiB of HBM per device.

v0:
```python
import jax
import jax.numpy as jnp
from jax import lax
from jax.sharding import PartitionSpec as P

ROPE_BASE = 10000.0
EPSILON = 1e-6


def rotate_half(vectors, cos_t, sin_t):
    half_dim = vectors.shape[-1] // 2
    lower_half = vectors[..., :half_dim]
    upper_half = vectors[..., half_dim:]
    return jnp.concatenate([lower_half * cos_t - upper_half * sin_t, upper_half * cos_t + lower_half * sin_t], axis=-1)


def project_token(hidden, w_norm, w_q, w_k, w_v, cache_len):
    head_dim = w_k.shape[1]
    num_heads = w_q.shape[1] // head_dim
    num_rows = hidden.shape[0]
    x_f32 = hidden.astype(jnp.float32)
    inv_rms = lax.rsqrt(jnp.mean(x_f32 * x_f32, axis=-1, keepdims=True) + EPSILON)
    x_norm = (x_f32 * inv_rms * (1.0 + w_norm.astype(jnp.float32))).astype(jnp.bfloat16)
    q_proj = jnp.dot(x_norm, w_q, preferred_element_type=jnp.float32).astype(jnp.bfloat16)
    k_proj = jnp.dot(x_norm, w_k, preferred_element_type=jnp.float32).astype(jnp.bfloat16)
    v_proj = jnp.dot(x_norm, w_v, preferred_element_type=jnp.float32).astype(jnp.bfloat16)
    inv_freq = ROPE_BASE ** (-jnp.arange(head_dim // 2, dtype=jnp.float32) * 2.0 / head_dim)
    angles = cache_len.astype(jnp.float32)[:, None] * inv_freq[None, :]
    cos_t = jnp.cos(angles)
    sin_t = jnp.sin(angles)
    q_heads = q_proj.astype(jnp.float32).reshape(num_rows, num_heads, head_dim)
    q_rot = (rotate_half(q_heads, cos_t[:, None, :], sin_t[:, None, :]) * head_dim ** -0.5).astype(jnp.bfloat16)
    k_rot = rotate_half(k_proj.astype(jnp.float32), cos_t, sin_t).astype(jnp.bfloat16)
    return x_f32, q_rot, k_rot, v_proj


def local_step(hidden, w_norm, w_q, w_k, w_v, w_o, k_block, v_block, cache_len):
    num_rows = hidden.shape[0]
    seq_block = k_block.shape[1]
    x_f32, q_rot, k_rot, v_proj = project_token(hidden, w_norm, w_q, w_k, w_v, cache_len)
    positions = lax.axis_index('sp') * seq_block + jnp.arange(seq_block)
    at_slot = (positions[None, :] == cache_len[:, None])[:, :, None]
    new_k_block = jnp.where(at_slot, k_rot[:, None, :], k_block)
    new_v_block = jnp.where(at_slot, v_proj[:, None, :], v_block)
    is_valid = (positions[None, :] <= cache_len[:, None])[:, None, :]
    scores = jnp.einsum('rhd,rtd->rht', q_rot, new_k_block, preferred_element_type=jnp.float32)
    masked = jnp.where(is_valid, scores, -jnp.inf)
    row_max = lax.pmax(jnp.max(masked, axis=-1), 'sp')
    weights = jnp.exp(masked - row_max[:, :, None])
    part_num = jnp.einsum('rht,rtd->rhd', weights.astype(jnp.bfloat16), new_v_block, preferred_element_type=jnp.float32)
    part_den = jnp.sum(weights, axis=-1)
    numerator, denominator = lax.psum((part_num, part_den), 'sp')
    attended = (numerator / denominator[:, :, None]).astype(jnp.bfloat16).reshape(num_rows, -1)
    out_hidden = x_f32 + jnp.dot(attended, w_o, preferred_element_type=jnp.float32)
    return out_hidden.astype(jnp.bfloat16), new_k_block, new_v_block


def solution(mesh):
    cache_spec = P('dp', 'sp', None)
    return jax.shard_map(local_step, mesh=mesh, in_specs=(P('dp', None), P(None), P(None, None), P(None, None), P(None, None), P(None, None), cache_spec, cache_spec, P('dp')), out_specs=(P('dp', None), cache_spec, cache_spec), check_vma=False)
```

profile of v0, /device:TPU:0, one launch (start us, length us, event | category | flops | bytes accessed | tf_op | source)
XLA Modules:
  0.0 223.1 jit_solution(16964192935511081195)
XLA Ops:
  7.2 0.0 copy-start
  7.2 0.0 copy-start.2
  7.2 0.0 all-reduce.2.cloned.1.call-start
  7.3 0.0 copy-start.5
  7.3 0.8 convert_element_type.46
  8.1 2.4 %fusion = f32[512]{0:T(512)S(1)} fusion(bf16[512,2048]{1,0:T(8,128)(2,1)} %param.9), kind=kLoop, calls=%fused_computation.5 | loop fusion | flops 3145216 | bytes 2099200 | tf_op jit(solution)/shard_map/reduce_sum | solution.py:22
  10.5 0.7 convert_add_fusion.1
  11.2 0.8 broadcast_compare_fusion.1
  12.1 0.0 copy-done
  12.1 3.1 %convolution_convert_fusion.1 = bf16[512,256]{1,0:T(8,128)(2,1)} fusion(bf16[2048,256]{1,0:T(8,128)(2,1)S(1)} %copy-done, bf16[512,2048]{1,0:T(8,128)(2,1)} %param.9, f32[2048]{0:T(1024)S(1)} %convert_add_fusion.1, f32[512]{0:T(512)S(1)} %add_rsqrt_fusion), kind=kOutput, calls=%fused_computation.22 | convolution fusion | flops 541196288 | bytes 3418112 | tf_op jit(solution)/shard_map/dot_general | solution.py:26
  15.1 0.0 copy-done.2
  15.1 0.0 copy-done.5
  15.1 0.9 fusion.11
  16.1 1.2 multiply_cosine_fusion
  17.3 0.1 copy.12
  17.4 0.1 copy.13
  17.6 0.1 copy.14
  17.7 7.0 %fusion.5 = f32[512,2048]{1,0:T(8,128)S(1)} fusion(bf16[2048,2048]{1,0:T(8,128)(2,1)} %param.11, bf16[512,2048]{1,0:T(8,128)(2,1)S(1)} %copy-done.2, f32[2048]{0:T(1024)S(1)} %convert_add_fusion.1, f32[512]{0:T(512)S(1)} %add_rsqrt_fusion), kind=kOutput, calls=%fused_computation.13 | convolution fusion | flops 4301258752 | bytes 14690304 | tf_op jit(solution)/shard_map/dot_general | solution.py:24
  24.7 2.0 copy.15
  26.7 0.0 copy-start.4
  26.7 2.5 %multiply_subtract_fusion = (f32[512,8,128]{2,1,0:T(8,128)}, f32[512,8,128]{2,1,0:T(8,128)}) fusion(f32[512,8,256]{2,1,0:T(8,128)S(1)} %bitcast.11, f32[512,128]{1,0:T(8,128)S(1)} %copy.13, f32[512,128]{1,0:T(8,128)S(1)} %copy.12), kind=kLoop, calls=%fused_computation.18 | loop fusion | flops 3145728 | bytes 8912896 | tf_op jit(solution)/shard_map/sub | solution.py:14
  29.2 0.0 copy-done.4
  29.2 44.4 %broadcast_select_fusion.1 = (bf16[512,128,256]{2,1,0:T(8,128)(2,1)}, bf16[512,128,256]{2,1,0:T(8,128)(2,1)}) fusion(bf16[512,128,256]{2,1,0:T(8,128)(2,1)} %param.15, pred[512,128]{1,0:T(8,128)(4,1)S(1)} %get-tuple-element.10, bf16[512,256]{1,0:T(8,128)(2,1)S(1)} %copy.14, bf16[512,128,256]{2,1,0:T(8,128)(2,1)} %param.16, bf16[512,256]{1,0:T(8,128)(2,1)S(1)} %copy-done.4), kind=kLoop, calls=%fused_computation.1 | loop fusion | flops 33554432 | bytes 134807552 | tf_op jit(solution)/shard_map/jit(_where)/select_n | solution.py:43
  73.6 15.6 %select_reduce_fusion = (f32[512,8]{1,0:T(8,128)S(1)}, f32[512,8,128]{2,1,0:T(8,128)S(1)}) fusion(pred[512,128]{1,0:T(8,128)(4,1)S(1)} %get-tuple-element.9, bf16[512,128,256]{2,1,0:T(8,128)(2,1)} %get-tuple-element.7, f32[512,8,128]{2,1,0:T(8,128)} %get-tuple-element.4, f32[512,8,128]{2,1,0:T(8,128)} %get-tuple-element.3), kind=kOutput, calls=%fused_computation.19 | convolution fusion | flops 272625664 | bytes 39927808 | tf_op jit(solution)/shard_map/rhd,rtd->rht/dot_general | solution.py:46
  89.2 28.0 %pmax.7 = f32[512,8]{1,0:T(8,128)S(1)} all-reduce(f32[512,8]{1,0:T(8,128)S(1)} %get-tuple-element.15), channel_id=1, replica_groups=mesh['dp'=1,'sp'=8] {'sp'}, use_global_device_ids=true, to_apply=%region_2.3 | all-reduce | flops 4096 | bytes 32768 | tf_op jit(solution)/shard_map/pmax | solution.py:48
  117.2 15.0 %fusion.12 = f32[512,8,256]{2,1,0:T(8,128)} fusion(bf16[512,128,256]{2,1,0:T(8,128)(2,1)} %get-tuple-element.8, f32[512,8,128]{2,1,0:T(8,128)S(1)} %get-tuple-element.16, f32[512,8]{1,0:T(8,128)S(1)} %pmax.7, pred[512,128]{1,0:T(8,128)(4,1)S(1)} %get-tuple-element.9), kind=kOutput, calls=%fused_computation.25 | convolution fusion | flops 270008320 | bytes 39927808 | tf_op jit(solution)/shard_map/rht,rtd->rhd/dot_general | solution.py:50
  132.2 0.0 all-reduce.2.cloned.1.call-update
  132.2 1.6 fusion.9
  133.8 27.5 %psum.15 = f32[512,8]{1,0:T(8,128)S(1)} all-reduce(f32[512,8]{1,0:T(8,128)S(1)} %fusion.9), channel_id=1, replica_groups=mesh['dp'=1,'sp'=8] {'sp'}, use_global_device_ids=true, to_apply=%region_5.6 | all-reduce | flops 4096 | bytes 32768 | tf_op jit(solution)/shard_map/psum | solution.py:52
  161.3 0.0 copy-start.3
  161.3 42.4 %all-reduce.2.cloned.1.call-done = f32[512,8,256]{2,1,0:T(8,128)} async-done(((f32[512,8,256]{2,1,0:T(8,128)}), f32[512,8,256]{2,1,0:T(8,128)}) %all-reduce.2.cloned.1.call-update) | async-done | bytes 4194320 | tf_op jit(solution)/shard_map/psum | solution.py:52
  203.7 2.6 %divide_convert_fusion = bf16[512,8,256]{2,1,0:T(8,128)(2,1)S(1)} fusion(f32[512,8,256]{2,1,0:T(8,128)} %all-reduce.2.cloned.1.call-done, f32[512,8]{1,0:T(8,128)S(1)} %psum.15), kind=kLoop, calls=%fused_computation.11 | loop fusion | flops 2097152 | bytes 6307840 | tf_op jit(solution)/shard_map/convert_element_type | solution.py:53
  206.3 0.7 copy.16
  207.0 0.0 copy-done.3
  207.0 0.0 copy-start.1
  207.0 9.2 %fusion.3 = bf16[512,2048]{1,0:T(8,128)(2,1)} fusion(bf16[512,2048]{1,0:T(8,128)(2,1)S(1)} %copy-done.3, bf16[512,2048]{1,0:T(8,128)(2,1)S(1)} %bitcast.14, bf16[2048,2048]{1,0:T(8,128)(2,1)} %param.14), kind=kOutput, calls=%fused_computation.8 | convolution fusion | flops 4298113024 | bytes 14680064 | tf_op jit(solution)/shard_map/dot_general | solution.py:54
  216.2 0.0 copy-done.1
  (4 shorter events, 0.0 us)
Async XLA Ops:
  7.2 4.9 %copy-start = (bf16[2048,256]{1,0:T(8,128)(2,1)S(1)}, bf16[2048,256]{1,0:T(8,128)(2,1)}, u32[]{:S(2)}) copy-start(bf16[2048,256]{1,0:T(8,128)(2,1)} %param.13) | copy-start | bytes 3145732
  7.2 8.0 %copy-start.2 = (bf16[512,2048]{1,0:T(8,128)(2,1)S(1)}, bf16[512,2048]{1,0:T(8,128)(2,1)}, u32[]{:S(2)}) copy-start(bf16[512,2048]{1,0:T(8,128)(2,1)} %param.9) | copy-start | bytes 6291460
  7.2 196.5 %all-reduce.2.cloned.1.call-start = ((), (), s32[]{:S(2)}) async-start(), calls=%async_computation | async-start | bytes 8388608 | tf_op jit(solution)/shard_map/psum | solution.py:52
  7.3 7.9 %copy-start.5 = (bf16[2048,256]{1,0:T(8,128)(2,1)S(1)}, bf16[2048,256]{1,0:T(8,128)(2,1)}, u32[]{:S(2)}) copy-start(bf16[2048,256]{1,0:T(8,128)(2,1)} %param.12) | copy-start | bytes 3145732
  26.7 2.6 %copy-start.4 = (bf16[512,256]{1,0:T(8,128)(2,1)S(1)}, bf16[512,256]{1,0:T(8,128)(2,1)}, u32[]{:S(2)}) copy-start(bf16[512,256]{1,0:T(8,128)(2,1)} %convolution_convert_fusion.1) | copy-start | bytes 786436
  161.3 45.7 %copy-start.3 = (bf16[512,2048]{1,0:T(8,128)(2,1)S(1)}, bf16[512,2048]{1,0:T(8,128)(2,1)}, u32[]{:S(2)}) copy-start(bf16[512,2048]{1,0:T(8,128)(2,1)} %param.9) | copy-start | bytes 6291460
  207.0 9.2 %copy-start.1 = (bf16[2048,256]{1,0:T(8,128)(2,1)S(1)}, bf16[2048,256]{1,0:T(8,128)(2,1)}, u32[]{:S(2)}) copy-start(bf16[2048,256]{1,0:T(8,128)(2,1)} %param.13) | copy-start | bytes 3145732
Sparse Core Ops, SparseCore 0:
  132.3 71.3 all-reduce.1
where the time goes:
time: 223 us
  other arithmetic  57.1 us (26%)
  blocking collectives  55.4 us (25%)
  matrix products  50.8 us (23%)
  waiting for transfers between devices  42.5 us (19%)
  between operations  14.2 us (6%)
  local copies, waits for them, and re-layouts  3.06 us (1%)
    select_n x1, other arithmetic, local_step(): new_k_block = jnp.where(at_slot, k_rot[:, None, :], k_block)  44.4 us
    psum x1, waiting for transfers between devices, local_step(): numerator, denominator = lax.psum((part_num, part_den), 'sp')  42.4 us
    pmax x1, blocking collectives, local_step(): row_max = lax.pmax(jnp.max(masked, axis=-1), 'sp')  28 us
    psum x1, blocking collectives, local_step(): numerator, denominator = lax.psum((part_num, part_den), 'sp')  27.5 us
    dot_general x1, matrix products, local_step(): jnp.einsum('rhd,rtd->rht', q_rot, new_k_block, preferred_element_type=jnp...  15.6 us
    dot_general x1, matrix products, local_step(): jnp.einsum('rht,rtd->rhd', weights.astype(jnp.bfloat16), new_v_block, pre...  15 us
    dot_general x1, matrix products, local_step(): jnp.dot(attended, w_o, preferred_element_type=jnp.float32)  9.23 us
    dot_general x1, matrix products, project_token(): jnp.dot(x_norm, w_q, preferred_element_type=jnp.float32)  6.99 us
  transfers between devices with their start and end apart: 1, of which 1 were waited for; matrix products, arithmetic and copies ran while one was open for 1% of the time, Pallas kernels for 0%

commit v1 on v0

v1 whole, which is shorter than its diff:
```python
import functools
import jax
import jax.numpy as jnp
from jax import lax
from jax.experimental import pallas as pl
from jax.experimental.pallas import tpu as pltpu
from jax.sharding import PartitionSpec as P

ROPE_BASE = 10000.0
EPSILON = 1e-6
F32 = jnp.float32
BF16 = jnp.bfloat16
LOWEST = -3.0e38
MESH_ID = pl.DeviceIdType.MESH

ROWS, D, HEADS, HEAD, SLOTS = 512, 2048, 8, 256, 128
CHUNK = 128
N_CHUNKS = ROWS // CHUNK
GROUP = 16
N_GROUPS = ROWS // GROUP
G_PER_CHUNK = CHUNK // GROUP
RING = 8
EIGHTH = CHUNK // 8


def place(me):
    core = me % 2
    x = (me // 2) % 2
    y = me // 4
    partner = me + 1 - 2 * core
    x_peer = me + 2 * (1 - 2 * x)
    y_peer = me + 4 * (1 - 2 * y)
    first_bit = x + core * (y - x)
    second_bit = y + core * (x - y)
    first_peer = x_peer + core * (y_peer - x_peer)
    second_peer = y_peer + core * (x_peer - y_peer)
    return core, first_bit, second_bit, partner, first_peer, second_peer


def eighth_of(me):
    core, first_bit, second_bit, _, _, _ = place(me)
    return core * 4 + first_bit * 2 + second_bit


def dot(a, b):
    return jnp.dot(a, b, preferred_element_type=F32)


def attend_kernel(x_ref, wn_ref, cos_ref, sin_ref, len_ref, wq_hbm, wk_hbm, wv_hbm, wo_hbm, k_hbm, v_hbm,
                  out_ref, knew_ref, vnew_ref,
                  w_buf, wkv_buf, xn_buf, q_buf, k_buf, v_buf, num_buf, stat_buf, d_recv, f_recv, s_recv,
                  d_stat, f_stat, s_stat, att_buf, w_sem, wkv_sem, k_sem, v_sem, send_sem, recv_sem, ssend_sem, srecv_sem):
    me = lax.axis_index('sp')
    core, first_bit, second_bit, partner, first_peer, second_peer = place(me)
    base = me * SLOTS

    def wq_copy(h):
        cols = pl.ds(pl.multiple_of(h * HEAD, HEAD), HEAD)
        return pltpu.make_async_copy(wq_hbm.at[:, cols], w_buf.at[:, cols], w_sem.at[h])

    def wo_copy(h):
        rows = pl.ds(pl.multiple_of(h * HEAD, HEAD), HEAD)
        return pltpu.make_async_copy(wo_hbm.at[rows, :], w_buf.at[rows, :], w_sem.at[h])

    def cache_copies(g):
        slot = g % RING
        rows = pl.ds(g * GROUP, GROUP)
        return (pltpu.make_async_copy(k_hbm.at[rows], k_buf.at[slot], k_sem.at[slot]),
                pltpu.make_async_copy(v_hbm.at[rows], v_buf.at[slot], v_sem.at[slot]))

    wk_copy = pltpu.make_async_copy(wk_hbm, wkv_buf.at[0], wkv_sem.at[0])
    wv_copy = pltpu.make_async_copy(wv_hbm, wkv_buf.at[1], wkv_sem.at[1])
    for h in range(2):
        wq_copy(h).start()
    wk_copy.start()
    wv_copy.start()
    for h in range(2, HEADS):
        wq_copy(h).start()
    for g in range(RING):
        for copy in cache_copies(g):
            copy.start()

    barrier = pltpu.get_barrier_semaphore()
    for peer in (partner, first_peer, second_peer):
        pl.semaphore_signal(barrier, inc=1, device_id={'sp': peer}, device_id_type=MESH_ID)
    pl.semaphore_wait(barrier, 3)

    gain = 1.0 + wn_ref[...].astype(F32)

    @pl.loop(0, ROWS // 16)
    def _(i):
        rows = pl.ds(pl.multiple_of(i * 16, 16), 16)
        x = x_ref[rows, :].astype(F32)
        inv = lax.rsqrt(jnp.mean(x * x, axis=-1, keepdims=True) + EPSILON)
        xn_buf[rows, :] = (x * inv * gain).astype(BF16)

    def rotate(u, rows):
        u = u.astype(BF16).astype(F32)
        c, s = cos_ref[rows, :], sin_ref[rows, :]
        lo, hi = u[:, :HEAD // 2], u[:, HEAD // 2:]
        return lo * c - hi * s, hi * c + lo * s

    half = HEAD // 2
    row_tiles = [pl.ds(t * 256, 256) for t in range(ROWS // 256)]

    @pl.loop(0, HEADS)
    def _(h):
        wq_copy(h).wait()
        cols = pl.ds(pl.multiple_of(h * HEAD, HEAD), HEAD)
        for t, rows in enumerate(row_tiles):
            lo, hi = rotate(dot(xn_buf[rows, :], w_buf[:, cols]), rows)
            dst = pl.ds(t * 256 * HEADS + h, 256, stride=HEADS)
            q_buf[0, dst, :] = lo * HEAD ** -0.5
            q_buf[1, dst, :] = hi * HEAD ** -0.5

    wk_copy.wait()
    for rows in row_tiles:
        lo, hi = rotate(dot(xn_buf[rows, :], wkv_buf[0]), rows)
        knew_ref[rows, :half] = lo.astype(BF16).astype(F32)
        knew_ref[rows, half:] = hi.astype(BF16).astype(F32)
    wv_copy.wait()
    for rows in row_tiles:
        vnew_ref[rows, :] = dot(xn_buf[rows, :], wkv_buf[1]).astype(BF16).astype(F32)

    for h in range(HEADS):
        wo_copy(h).start()

    lane = lax.broadcasted_iota(jnp.int32, (HEADS, SLOTS), 1)
    sub16 = lax.broadcasted_iota(jnp.int32, (16, HEAD), 0).astype(F32).astype(BF16)

    def patched(ref, slot, j, new_row, lim):
        new = jnp.broadcast_to(new_row, (16, HEAD)).astype(BF16)
        tiles = []
        for t in range(SLOTS // 16):
            at = jnp.full((16, HEAD), (lim - t * 16).astype(F32), F32).astype(BF16)
            tiles.append(jnp.where(sub16 == at, new, ref[slot, j, t * 16:(t + 1) * 16, :]))
        return jnp.concatenate(tiles, axis=0)

    def attend_group(g):
        slot = g % RING
        for copy in cache_copies(g):
            copy.wait()
        chunk = g // G_PER_CHUNK
        m_tile = stat_buf[chunk, 0]
        d_tile = stat_buf[chunk, 1]
        for pair in range(GROUP // 2):
            r0 = g * GROUP + 2 * pair
            lims = [len_ref[r0 + a] - base for a in range(2)]
            keys = jnp.concatenate([patched(k_buf, slot, 2 * pair + a, knew_ref[pl.ds(r0 + a, 1), :], lims[a]) for a in range(2)], axis=0)
            q_rows = pl.ds(pl.multiple_of(r0 * HEADS, 16), 16)
            q2 = jnp.concatenate([q_buf[0, q_rows, :], q_buf[1, q_rows, :]], axis=1).astype(BF16)
            s2 = lax.dot_general(q2, keys, (((1,), (1,)), ((), ())), preferred_element_type=F32)
            probs = []
            for a in range(2):
                s = s2[a * HEADS:(a + 1) * HEADS, a * SLOTS:(a + 1) * SLOTS]
                valid = lane <= lims[a]
                m = jnp.max(jnp.where(valid, s, LOWEST), axis=-1, keepdims=True)
                p = jnp.where(valid, jnp.exp(s - m), 0.0)
                den = jnp.sum(p, axis=-1, keepdims=True)
                here = lane == (g % G_PER_CHUNK) * GROUP + 2 * pair + a
                m_tile = jnp.where(here, m, m_tile)
                d_tile = jnp.where(here, den, d_tile)
                probs.append(p)
            zero = jnp.zeros((HEADS, SLOTS), F32)
            p2 = jnp.concatenate([jnp.concatenate([probs[0], zero], axis=1), jnp.concatenate([zero, probs[1]], axis=1)], axis=0).astype(BF16)
            values = jnp.concatenate([patched(v_buf, slot, 2 * pair + a, vnew_ref[pl.ds(r0 + a, 1), :], lims[a]) for a in range(2)], axis=0)
            num_buf[pl.ds(pl.multiple_of(r0 * HEADS, 16), 16), :] = dot(p2, values)
        stat_buf[chunk, 0] = m_tile
        stat_buf[chunk, 1] = d_tile

        @pl.when(g + RING < N_GROUPS)
        def _():
            for copy in cache_copies(g + RING):
                copy.start()

    def num_rows(k, offset, count):
        return pl.ds(pl.multiple_of((k * CHUNK + offset) * HEADS, 128), count * HEADS)

    half_rows, quarter_rows = CHUNK // 2, CHUNK // 4
    my_half = core * half_rows
    my_quarter = my_half + first_bit * quarter_rows
    my_eighth = my_quarter + second_bit * EIGHTH

    def exchange(stage, k):
        recv, stat, peer, offset, count = (
            (d_recv, d_stat, partner, (1 - core) * half_rows, half_rows),
            (f_recv, f_stat, first_peer, my_half + (1 - first_bit) * quarter_rows, quarter_rows),
            (s_recv, s_stat, second_peer, my_quarter + (1 - second_bit) * EIGHTH, EIGHTH))[stage]
        return (pltpu.make_async_remote_copy(
                    src_ref=num_buf.at[num_rows(k, offset, count), :], dst_ref=recv.at[k],
                    send_sem=send_sem.at[stage, k], recv_sem=recv_sem.at[stage, k],
                    device_id={'sp': peer}, device_id_type=MESH_ID),
                pltpu.make_async_remote_copy(
                    src_ref=stat_buf.at[stage * N_CHUNKS + k], dst_ref=stat.at[k],
                    send_sem=ssend_sem.at[stage, k], recv_sem=srecv_sem.at[stage, k],
                    device_id={'sp': peer}, device_id_type=MESH_ID))

    def merge(stage, k):
        recv, stat, offset, count = (
            (d_recv, d_stat, my_half, half_rows),
            (f_recv, f_stat, my_quarter, quarter_rows),
            (s_recv, s_stat, my_eighth, EIGHTH))[stage]
        for copy in exchange(stage, k):
            copy.wait_recv()
        m_a, d_a = stat_buf[stage * N_CHUNKS + k, 0], stat_buf[stage * N_CHUNKS + k, 1]
        m_b, d_b = stat[k, 0], stat[k, 1]
        m = jnp.maximum(m_a, m_b)
        f_a, f_b = jnp.exp(m_a - m), jnp.exp(m_b - m)
        den = d_a * f_a + d_b * f_b
        last = stage == 2
        if last:
            f_a, f_b = f_a / den, f_b / den
        else:
            stat_buf[(stage + 1) * N_CHUNKS + k, 0] = m
            stat_buf[(stage + 1) * N_CHUNKS + k, 1] = den
        shift = (CHUNK - offset) % CHUNK
        f_a = pltpu.roll(f_a, shift, 1)
        f_b = pltpu.roll(f_b, shift, 1)
        start = (k * CHUNK + offset) * HEADS
        for r in range(count):
            dst = pl.ds(pl.multiple_of(start + r * HEADS, HEADS), HEADS)
            total = num_buf[dst, :] * f_a[:, r:r + 1] + recv[k, r * HEADS:(r + 1) * HEADS, :] * f_b[:, r:r + 1]
            if last:
                att_buf[0, r * HEADS:(r + 1) * HEADS, :] = total[:, :half]
                att_buf[1, r * HEADS:(r + 1) * HEADS, :] = total[:, half:]
            else:
                num_buf[dst, :] = total

    def send(stage, k):
        for copy in exchange(stage, k):
            copy.start()

    def project_out(k):
        atts = []
        for h in range(HEADS):
            heads = pl.ds(h, EIGHTH, stride=HEADS)
            atts.append(jnp.concatenate([att_buf[0, heads, :], att_buf[1, heads, :]], axis=1).astype(BF16))
        x_rows = pl.ds(pl.multiple_of(k * CHUNK + my_eighth, EIGHTH), EIGHTH)
        o_rows = pl.ds(pl.multiple_of(k * EIGHTH, EIGHTH), EIGHTH)
        for n in range(D // 512):
            cols = slice(n * 512, (n + 1) * 512)
            acc = dot(atts[0], w_buf[0:HEAD, cols])
            for h in range(1, HEADS):
                acc += dot(atts[h], w_buf[h * HEAD:(h + 1) * HEAD, cols])
            out_ref[o_rows, cols] = (x_ref[x_rows, cols].astype(F32) + acc).astype(BF16).astype(F32)

    @pl.loop(0, N_CHUNKS + 3)
    def _(t):
        @pl.when(t < N_CHUNKS)
        def _():
            @pl.loop(0, G_PER_CHUNK // 2)
            def _(i):
                attend_group(t * G_PER_CHUNK + i)

        @pl.when((t >= 1) & (t < N_CHUNKS + 1))
        def _():
            merge(0, t - 1)
            send(1, t - 1)

        @pl.when((t >= 2) & (t < N_CHUNKS + 2))
        def _():
            merge(1, t - 2)
            send(2, t - 2)

        @pl.when(t >= 3)
        def _():
            @pl.when(t == 3)
            def _():
                for h in range(HEADS):
                    wo_copy(h).wait()
            merge(2, t - 3)
            project_out(t - 3)

        @pl.when(t < N_CHUNKS)
        def _():
            @pl.loop(G_PER_CHUNK // 2, G_PER_CHUNK)
            def _(i):
                attend_group(t * G_PER_CHUNK + i)
            send(0, t)

    @pl.loop(0, N_CHUNKS)
    def _(k):
        for stage in range(3):
            for copy in exchange(stage, k):
                copy.wait_send()


def attend(hidden, w_norm, cos_t, sin_t, cache_len, w_q, w_k, w_v, w_o, k_block, v_block):
    vmem = pl.BlockSpec(memory_space=pltpu.VMEM)
    hbm = pl.BlockSpec(memory_space=pl.ANY)
    return pl.pallas_call(
        attend_kernel,
        out_shape=(jax.ShapeDtypeStruct((ROWS // 8, D), F32), jax.ShapeDtypeStruct((ROWS, HEAD), F32), jax.ShapeDtypeStruct((ROWS, HEAD), F32)),
        in_specs=[vmem, vmem, vmem, vmem, pl.BlockSpec(memory_space=pltpu.SMEM)] + [hbm] * 6,
        out_specs=(vmem, vmem, vmem),
        scratch_shapes=[
            pltpu.VMEM((D, D), BF16), pltpu.VMEM((2, D, HEAD), BF16), pltpu.VMEM((ROWS, D), BF16),
            pltpu.VMEM((2, ROWS * HEADS, HEAD // 2), F32),
            pltpu.VMEM((RING, GROUP, SLOTS, HEAD), BF16), pltpu.VMEM((RING, GROUP, SLOTS, HEAD), BF16),
            pltpu.VMEM((ROWS * HEADS, HEAD), F32), pltpu.VMEM((3 * N_CHUNKS, 2, HEADS, CHUNK), F32),
            pltpu.VMEM((N_CHUNKS, CHUNK // 2 * HEADS, HEAD), F32),
            pltpu.VMEM((N_CHUNKS, CHUNK // 4 * HEADS, HEAD), F32),
            pltpu.VMEM((N_CHUNKS, EIGHTH * HEADS, HEAD), F32),
            pltpu.VMEM((N_CHUNKS, 2, HEADS, CHUNK), F32), pltpu.VMEM((N_CHUNKS, 2, HEADS, CHUNK), F32), pltpu.VMEM((N_CHUNKS, 2, HEADS, CHUNK), F32),
            pltpu.VMEM((2, EIGHTH * HEADS, HEAD // 2), F32),
            pltpu.SemaphoreType.DMA((HEADS,)), pltpu.SemaphoreType.DMA((2,)),
            pltpu.SemaphoreType.DMA((RING,)), pltpu.SemaphoreType.DMA((RING,)),
            pltpu.SemaphoreType.DMA((3, N_CHUNKS)), pltpu.SemaphoreType.DMA((3, N_CHUNKS)),
            pltpu.SemaphoreType.DMA((3, N_CHUNKS)), pltpu.SemaphoreType.DMA((3, N_CHUNKS)),
        ],
        compiler_params=pltpu.CompilerParams(collective_id=0, has_side_effects=True, vmem_limit_bytes=60 * 2 ** 20),
        cost_estimate=pl.CostEstimate(flops=20 * 10 ** 9, bytes_accessed=90 * 10 ** 6, transcendentals=0),
    )(hidden, w_norm, cos_t, sin_t, cache_len, w_q, w_k, w_v, w_o, k_block, v_block)


COPY_RING = 8


def cache_kernel(len_ref, knew_ref, vnew_ref, k_hbm, v_hbm, ko_hbm, vo_hbm, buf, in_sem, out_sem):
    base = lax.axis_index('sp') * SLOTS
    sub16 = lax.broadcasted_iota(jnp.int32, (16, HEAD), 0)

    def ins(g):
        slot, rows = g % COPY_RING, pl.ds(g * GROUP, GROUP)
        return [pltpu.make_async_copy(src.at[rows], buf.at[i, slot], in_sem.at[i, slot]) for i, src in enumerate((k_hbm, v_hbm))]

    def outs(g):
        slot, rows = g % COPY_RING, pl.ds(g * GROUP, GROUP)
        return [pltpu.make_async_copy(buf.at[i, slot], dst.at[rows], out_sem.at[i, slot]) for i, dst in enumerate((ko_hbm, vo_hbm))]

    ahead = COPY_RING // 2
    for g in range(ahead):
        for copy in ins(g):
            copy.start()

    @pl.loop(0, N_GROUPS)
    def _(g):
        @pl.when(g + ahead < N_GROUPS)
        def _():
            @pl.when(g + ahead >= COPY_RING)
            def _():
                for copy in outs(g + ahead - COPY_RING):
                    copy.wait()
            for copy in ins(g + ahead):
                copy.start()
        for copy in ins(g):
            copy.wait()
        slot = g % COPY_RING
        for j in range(GROUP):
            r = g * GROUP + j
            at = len_ref[r] - base
            tile = jnp.clip(at, 0, SLOTS - 1) // 16 * 16
            span = pl.ds(pl.multiple_of(tile, 16), 16)
            hit = sub16 == at - tile
            for i, new_ref in enumerate((knew_ref, vnew_ref)):
                new = jnp.broadcast_to(new_ref[pl.ds(r, 1), :], (16, HEAD))
                old = buf[i, slot, j, span, :].astype(F32)
                buf[i, slot, j, span, :] = jnp.where(hit, new, old).astype(BF16)
        for copy in outs(g):
            copy.start()

    @pl.loop(N_GROUPS - COPY_RING, N_GROUPS)
    def _(g):
        for copy in outs(g):
            copy.wait()


def update_caches(cache_len, k_new, v_new, k_block, v_block):
    vmem = pl.BlockSpec(memory_space=pltpu.VMEM)
    hbm = pl.BlockSpec(memory_space=pl.ANY)
    shape = jax.ShapeDtypeStruct(k_block.shape, k_block.dtype)
    return pl.pallas_call(
        cache_kernel,
        out_shape=(shape, shape),
        in_specs=[pl.BlockSpec(memory_space=pltpu.SMEM), vmem, vmem, hbm, hbm],
        out_specs=(hbm, hbm),
        scratch_shapes=[pltpu.VMEM((2, COPY_RING, GROUP, SLOTS, HEAD), BF16), pltpu.SemaphoreType.DMA((2, COPY_RING)), pltpu.SemaphoreType.DMA((2, COPY_RING))],
        compiler_params=pltpu.CompilerParams(vmem_limit_bytes=40 * 2 ** 20),
        cost_estimate=pl.CostEstimate(flops=20 * 10 ** 9, bytes_accessed=134 * 10 ** 6, transcendentals=0),
    )(cache_len, k_new, v_new, k_block, v_block)


PIECES = (0, 2, 4, 6, 1, 3, 5, 7)


def assemble_kernel(*refs):
    pieces, out_ref = refs[:8], refs[8]
    me = lax.axis_index('sp')
    core, x, y = me % 2, (me // 2) % 2, me // 4
    for piece, flip in zip(pieces, PIECES):
        c = core + (flip % 2) * (1 - 2 * core)
        px = x + (flip // 2 % 2) * (1 - 2 * x)
        py = y + (flip // 4) * (1 - 2 * y)
        e = eighth_of(py * 4 + px * 2 + c)
        out_ref[pl.ds(pl.multiple_of(e * EIGHTH, EIGHTH), EIGHTH), :] = piece[...].astype(BF16)


def assemble(pieces):
    return pl.pallas_call(
        assemble_kernel,
        grid=(N_CHUNKS,),
        out_shape=jax.ShapeDtypeStruct((ROWS, D), BF16),
        in_specs=[pl.BlockSpec((EIGHTH, D), lambda k: (k, 0))] * 8,
        out_specs=pl.BlockSpec((CHUNK, D), lambda k: (k, 0)),
        cost_estimate=pl.CostEstimate(flops=10 ** 9, bytes_accessed=6 * 2 ** 20, transcendentals=0),
    )(*pieces)


def local_step(hidden, w_norm, w_q, w_k, w_v, w_o, k_block, v_block, cache_len):
    inv_freq = ROPE_BASE ** (-jnp.arange(HEAD // 2, dtype=F32) * 2.0 / HEAD)
    angles = cache_len.astype(F32)[:, None] * inv_freq[None, :]
    own, k_new, v_new = attend(hidden, w_norm[None, :], jnp.cos(angles), jnp.sin(angles), cache_len, w_q, w_k, w_v, w_o, k_block, v_block)

    def flip(array, bits):
        return lax.ppermute(array, 'sp', [(i, i ^ bits) for i in range(8)])

    held = [own] + [flip(own, bits) for bits in (2, 4, 6)]
    new_k, new_v = update_caches(cache_len, k_new, v_new, k_block, v_block)
    other = [flip(piece, 1) for piece in held]
    return assemble(held + other), new_k, new_v


def solution(mesh):
    cache_spec = P('dp', 'sp', None)
    return jax.shard_map(local_step, mesh=mesh, in_specs=(P('dp', None), P(None), P(None, None), P(None, None), P(None, None), P(None, None), cache_spec, cache_spec, P('dp')), out_specs=(P('dp', None), cache_spec, cache_spec), check_vma=False)
```

time: 223 us -> 192 us (0.86)
  Pallas kernels: 0 us -> 159 us
  blocking collectives: 55.4 us -> 0 us
  other arithmetic: 57.1 us -> 2.49 us
  matrix products: 50.8 us -> 0 us
  waiting for transfers between devices: 42.5 us -> 21.7 us
  between operations: 14.2 us -> 0.74 us
  starting transfers between devices: 0.04 us -> 3.79 us
    pallas_call x0 -> x3, Pallas kernels: none -> 159 us  [the longest x1 109 us: attend(): pl.pallas_call(attend_kernel, out_shape=(jax.ShapeDtypeStruct((ROWS // 8,...]
    dot_general x6 -> x0, matrix products: 50.8 us -> none  [the longest x1 15.6 us: local_step(): jnp.einsum('rhd,rtd->rht', q_rot, new_k_block, preferred_element_type=jnp...]
    select_n x1 -> x0, other arithmetic: 44.4 us -> none  [local_step(): new_k_block = jnp.where(at_slot, k_rot[:, None, :], k_block)]
    psum x1 -> x0, waiting for transfers between devices: 42.4 us -> none  [local_step(): numerator, denominator = lax.psum((part_num, part_den), 'sp')]
    pmax x1 -> x0, blocking collectives: 28 us -> none  [local_step(): row_max = lax.pmax(jnp.max(masked, axis=-1), 'sp')]
    psum x1 -> x0, blocking collectives: 27.5 us -> none  [local_step(): numerator, denominator = lax.psum((part_num, part_den), 'sp')]
    ppermute x0 -> x7, waiting for transfers between devices: none -> 21.7 us  [flip(): return lax.ppermute(array, 'sp', [(i, i ^ bits) for i in range(8)])]
    reduce_sum x2 -> x0, other arithmetic: 3.98 us -> none  [the longest x1 2.4 us: project_token(): jnp.mean(x_f32 * x_f32, axis=-1, keepdims=True) + EPSILON]
  transfers between devices with their start and end apart: 1 -> 7, of which waited for: 1 -> 3; matrix products, arithmetic and copies ran while one was open for 1% -> 0% of each run, Pallas kernels for 0% -> 24%
where the time goes in v1:
time: 192 us
  Pallas kernels  159 us (83%)
  waiting for transfers between devices  21.7 us (11%)
  local copies, waits for them, and re-layouts  4.5 us (2%)
  starting transfers between devices  3.79 us (2%)
  other arithmetic  2.49 us (1%)
    pallas_call x1, Pallas kernels, attend(): pl.pallas_call(attend_kernel, out_shape=(jax.ShapeDtypeStruct((ROWS // 8,...  109 us
    pallas_call x1, Pallas kernels, update_caches(): pl.pallas_call(cache_kernel, out_shape=(shape, shape), in_specs=[pl.Block...  45.2 us
    ppermute x7, waiting for transfers between devices, flip(): return lax.ppermute(array, 'sp', [(i, i ^ bits) for i in range(8)])  21.7 us
    pallas_call x1, Pallas kernels, assemble(): pl.pallas_call(assemble_kernel, grid=(N_CHUNKS,), out_shape=jax.ShapeDtyp...  4.54 us
  transfers between devices with their start and end apart: 7, of which 3 were waited for; matrix products, arithmetic and copies ran while one was open for 0% of the time, Pallas kernels for 24%

profile of v1, /device:TPU:0, one launch (start us, length us, event | category | flops | bytes accessed | tf_op | source)
XLA Modules:
  0.0 191.8 jit_solution(9657329146894008125)
XLA Ops:
  0.6 0.7 convert_element_type.3
  1.3 1.3 broadcast_in_dim.2.wn_ref
  2.6 1.8 multiply_sine_fusion
  4.4 0.0 copy-start
  4.4 109.0 %shard_map.112 = (f32[64,2048]{1,0:T(8,128)}, f32[512,256]{1,0:T(8,128)}, f32[512,256]{1,0:T(8,128)}) custom-call(bf16[512,2048]{1,0:T(8,128)(2,1)} %x_ref.1, bf16[1,2048]{1,0:T(2,128)(2,1)} %broadcast_in_dim.2.wn_ref, f32[512,128]{1,0:T(8,128)} %get-tuple-element.14.cos_ref, f32[512,128]{1,0:T(8,128)} %get-tuple-element.13.sin_ref, s32[512]{0:T(512)} %len_ref.3, ...), custom_call_target="tpu_custom_call" | custom-call | flops 20000000000 | bytes 90000000 | tf_op jit(solution)/shard_map/pallas_call | solution.py:291
  113.4 1.1 collective-permute-start.2
  114.5 1.5 collective-permute-start.1
  116.0 1.0 collective-permute-start
  116.9 0.0 collective-permute-start.3
  116.9 12.3 %collective-permute-done.2.refs_3_ = f32[64,2048]{1,0:T(8,128)S(1)} collective-permute-done((f32[64,2048]{1,0:T(8,128)}, f32[64,2048]{1,0:T(8,128)S(1)}, u32[]{:S(2)}, u32[]{:S(2)}) %collective-permute-start.2) | collective-permute-done | bytes 524320 | tf_op jit(solution)/shard_map/ppermute | solution.py:415
  129.2 0.0 copy-start.3
  129.2 0.0 collective-permute-start.6
  129.2 9.1 %collective-permute-done.1.refs_2_ = f32[64,2048]{1,0:T(8,128)S(1)} collective-permute-done((f32[64,2048]{1,0:T(8,128)}, f32[64,2048]{1,0:T(8,128)S(1)}, u32[]{:S(2)}, u32[]{:S(2)}) %collective-permute-start.1) | collective-permute-done | bytes 524320 | tf_op jit(solution)/shard_map/ppermute | solution.py:415
  138.3 0.0 copy-start.4
  138.3 0.0 collective-permute-start.5
  138.3 0.2 collective-permute-done.refs_1_
  138.6 0.0 copy-start.5
  138.6 0.3 collective-permute-start.4
  138.8 0.0 copy-done
  138.8 0.0 copy-start.1
  138.8 1.0 copy-done.1
  139.9 0.0 copy-start.2
  139.9 1.0 copy-done.2
  140.9 45.2 %shard_map.114 = (bf16[512,128,256]{2,1,0:T(8,128)(2,1)}, bf16[512,128,256]{2,1,0:T(8,128)(2,1)}) custom-call(s32[512]{0:T(512)S(1)} %copy-done, f32[512,256]{1,0:T(8,128)S(1)} %copy-done.1, f32[512,256]{1,0:T(8,128)S(1)} %copy-done.2, bf16[512,128,256]{2,1,0:T(8,128)(2,1)} %k_hbm.3, bf16[512,128,256]{2,1,0:T(8,128)(2,1)} %v_hbm.3), custom_call_target="tpu_custom_call" | custom-call | flops 20000000000 | bytes 134000000 | tf_op jit(solution)/shard_map/pallas_call | solution.py:372
  186.1 0.0 copy-done.3
  186.1 0.0 copy-done.4
  186.1 0.0 copy-done.5
  186.1 0.0 collective-permute-done.3.refs_4_
  186.1 0.0 copy-start.6
  186.1 0.0 collective-permute-done.6.refs_7_
  186.2 0.0 copy-start.7
  186.2 0.0 collective-permute-done.5.refs_6_
  186.2 0.0 copy-start.8
  186.2 0.0 collective-permute-done.4.refs_5_
  186.2 0.7 copy-done.6
  186.9 0.2 copy-done.7
  187.1 0.2 copy-done.8
  187.3 4.5 %shard_map.113 = bf16[512,2048]{1,0:T(8,128)(2,1)} custom-call(f32[64,2048]{1,0:T(8,128)} %get-tuple-element.8.refs_0_, f32[64,2048]{1,0:T(8,128)} %copy-done.5, f32[64,2048]{1,0:T(8,128)} %copy-done.4, f32[64,2048]{1,0:T(8,128)} %copy-done.3, f32[64,2048]{1,0:T(8,128)} %copy-done.6, f32[64,2048]{1,0:T(8,128)} %collective-permute-done.4.refs_5_, ...), custom_call_target="tpu_custom_call" | custom-call | flops 1000000000 | bytes 6291456 | tf_op jit(solution)/shard_map/pallas_call | solution.py:399
  (1 shorter events, 0.0 us)
Async XLA Ops:
  4.4 134.4 %copy-start = (s32[512]{0:T(512)S(1)}, s32[512]{0:T(512)}, u32[]{:S(2)}) copy-start(s32[512]{0:T(512)} %len_ref.3) | copy-start | bytes 6148
  113.4 15.8 %collective-permute-start.2 = (f32[64,2048]{1,0:T(8,128)}, f32[64,2048]{1,0:T(8,128)S(1)}, u32[]{:S(2)}, u32[]{:S(2)}) collective-permute-start(f32[64,2048]{1,0:T(8,128)} %get-tuple-element.8.refs_0_), channel_id=1, source_target_pairs={{0,6},{1,7},{2,4},{3,5},{4,2},{5,3},{6,0},{7,1}} | collective-permute-start | bytes 1572872 | tf_op jit(solution)/shard_map/ppermute | solution.py:415
  114.5 23.9 %collective-permute-start.1 = (f32[64,2048]{1,0:T(8,128)}, f32[64,2048]{1,0:T(8,128)S(1)}, u32[]{:S(2)}, u32[]{:S(2)}) collective-permute-start(f32[64,2048]{1,0:T(8,128)} %get-tuple-element.8.refs_0_), channel_id=1, source_target_pairs={{0,4},{1,5},{2,6},{3,7},{4,0},{5,1},{6,2},{7,3}} | collective-permute-start | bytes 1572872 | tf_op jit(solution)/shard_map/ppermute | solution.py:415
  116.0 22.6 %collective-permute-start = (f32[64,2048]{1,0:T(8,128)}, f32[64,2048]{1,0:T(8,128)S(1)}, u32[]{:S(2)}, u32[]{:S(2)}) collective-permute-start(f32[64,2048]{1,0:T(8,128)} %get-tuple-element.8.refs_0_), channel_id=1, source_target_pairs={{0,2},{1,3},{2,0},{3,1},{4,6},{5,7},{6,4},{7,5}} | collective-permute-start | bytes 1572872 | tf_op jit(solution)/shard_map/ppermute | solution.py:415
  116.9 69.2 %collective-permute-start.3 = (f32[64,2048]{1,0:T(8,128)}, f32[64,2048]{1,0:T(8,128)S(1)}, u32[]{:S(2)}, u32[]{:S(2)}) collective-permute-start(f32[64,2048]{1,0:T(8,128)} %get-tuple-element.8.refs_0_), channel_id=1, source_target_pairs={{0,1},{1,0},{2,3},{3,2},{4,5},{5,4},{6,7},{7,6}} | collective-permute-start | bytes 1572872 | tf_op jit(solution)/shard_map/ppermute | solution.py:415
  129.2 56.9 %copy-start.3 = (f32[64,2048]{1,0:T(8,128)}, f32[64,2048]{1,0:T(8,128)S(1)}, u32[]{:S(2)}) copy-start(f32[64,2048]{1,0:T(8,128)S(1)} %collective-permute-done.2.refs_3_) | copy-start | bytes 1572868
  129.2 56.9 %collective-permute-start.6 = (f32[64,2048]{1,0:T(8,128)S(1)}, f32[64,2048]{1,0:T(8,128)S(1)}, u32[]{:S(2)}, u32[]{:S(2)}) collective-permute-start(f32[64,2048]{1,0:T(8,128)S(1)} %collective-permute-done.2.refs_3_), channel_id=1, source_target_pairs={{0,1},{1,0},{2,3},{3,2},{4,5},{5,4},{6,7},{7,6}} | collective-permute-start | bytes 1572872 | tf_op jit(solution)/shard_map/ppermute | solution.py:415
  138.3 47.8 %copy-start.4 = (f32[64,2048]{1,0:T(8,128)}, f32[64,2048]{1,0:T(8,128)S(1)}, u32[]{:S(2)}) copy-start(f32[64,2048]{1,0:T(8,128)S(1)} %collective-permute-done.1.refs_2_) | copy-start | bytes 1572868
  138.3 47.8 %collective-permute-start.5 = (f32[64,2048]{1,0:T(8,128)S(1)}, f32[64,2048]{1,0:T(8,128)S(1)}, u32[]{:S(2)}, u32[]{:S(2)}) collective-permute-start(f32[64,2048]{1,0:T(8,128)S(1)} %collective-permute-done.1.refs_2_), channel_id=1, source_target_pairs={{0,1},{1,0},{2,3},{3,2},{4,5},{5,4},{6,7},{7,6}} | collective-permute-start | bytes 1572872 | tf_op jit(solution)/shard_map/ppermute | solution.py:415
  138.6 47.5 %copy-start.5 = (f32[64,2048]{1,0:T(8,128)}, f32[64,2048]{1,0:T(8,128)S(1)}, u32[]{:S(2)}) copy-start(f32[64,2048]{1,0:T(8,128)S(1)} %collective-permute-done.refs_1_) | copy-start | bytes 1572868
  138.6 47.6 %collective-permute-start.4 = (f32[64,2048]{1,0:T(8,128)S(1)}, f32[64,2048]{1,0:T(8,128)}, u32[]{:S(2)}, u32[]{:S(2)}) collective-permute-start(f32[64,2048]{1,0:T(8,128)S(1)} %collective-permute-done.refs_1_), channel_id=1, source_target_pairs={{0,1},{1,0},{2,3},{3,2},{4,5},{5,4},{6,7},{7,6}} | collective-permute-start | bytes 1572872 | tf_op jit(solution)/shard_map/ppermute | solution.py:415
  138.8 1.0 copy-start.1
  139.9 1.0 copy-start.2
  186.1 0.8 copy-start.6
  186.2 1.0 copy-start.7
  186.2 1.1 copy-start.8

commit v2 on v1

--- a/solution.py
+++ b/solution.py
@@ -1,6 +1,7 @@
 import functools
 import jax
 import jax.numpy as jnp
+import numpy as np
 from jax import lax
 from jax.experimental import pallas as pl
 from jax.experimental.pallas import tpu as pltpu
@@ -19,8 +20,9 @@
 GROUP = 16
 N_GROUPS = ROWS // GROUP
 G_PER_CHUNK = CHUNK // GROUP
-RING = 8
+RING = 16
 EIGHTH = CHUNK // 8
+X_ROWS = 128
 
 
 def place(me):
@@ -46,10 +48,10 @@
     return jnp.dot(a, b, preferred_element_type=F32)
 
 
-def attend_kernel(x_ref, wn_ref, cos_ref, sin_ref, len_ref, wq_hbm, wk_hbm, wv_hbm, wo_hbm, k_hbm, v_hbm,
-                  out_ref, knew_ref, vnew_ref,
-                  w_buf, wkv_buf, xn_buf, q_buf, k_buf, v_buf, num_buf, stat_buf, d_recv, f_recv, s_recv,
-                  d_stat, f_stat, s_stat, att_buf, w_sem, wkv_sem, k_sem, v_sem, send_sem, recv_sem, ssend_sem, srecv_sem):
+def attend_kernel(len_ref, freq_ref, wn_ref, x_hbm, wq_hbm, wk_hbm, wv_hbm, wo_hbm, k_hbm, v_hbm,
+                  out_ref, knew_ref, vnew_ref, k_buf, v_buf,
+                  w_buf, wkv_buf, xn_buf, x_own, cos_ref, sin_ref, q_buf, stat_buf, d_recv, f_recv, s_recv,
+                  d_stat, f_stat, s_stat, p_buf, x_sem, own_sem, w_sem, wkv_sem, k_sem, v_sem, send_sem, recv_sem, ssend_sem, srecv_sem):
     me = lax.axis_index('sp')
     core, first_bit, second_bit, partner, first_peer, second_peer = place(me)
     base = me * SLOTS
@@ -68,6 +70,16 @@
         return (pltpu.make_async_copy(k_hbm.at[rows], k_buf.at[slot], k_sem.at[slot]),
                 pltpu.make_async_copy(v_hbm.at[rows], v_buf.at[slot], v_sem.at[slot]))
 
+    def x_copy(i):
+        rows = pl.ds(i * X_ROWS, X_ROWS)
+        return pltpu.make_async_copy(x_hbm.at[rows, :], xn_buf.at[rows, :], x_sem.at[i])
+
+    def own_copy(k):
+        rows = pl.ds(pl.multiple_of(k * CHUNK + eighth_of(me) * EIGHTH, EIGHTH), EIGHTH)
+        return pltpu.make_async_copy(x_hbm.at[rows, :], x_own.at[k], own_sem.at[k])
+
+    for i in range(ROWS // X_ROWS):
+        x_copy(i).start()
     wk_copy = pltpu.make_async_copy(wk_hbm, wkv_buf.at[0], wkv_sem.at[0])
     wv_copy = pltpu.make_async_copy(wv_hbm, wkv_buf.at[1], wkv_sem.at[1])
     for h in range(2):
@@ -76,6 +88,8 @@
     wv_copy.start()
     for h in range(2, HEADS):
         wq_copy(h).start()
+    for k in range(N_CHUNKS):
+        own_copy(k).start()
     for g in range(RING):
         for copy in cache_copies(g):
             copy.start()
@@ -85,14 +99,31 @@
         pl.semaphore_signal(barrier, inc=1, device_id={'sp': peer}, device_id_type=MESH_ID)
     pl.semaphore_wait(barrier, 3)
 
-    gain = 1.0 + wn_ref[...].astype(F32)
-
     @pl.loop(0, ROWS // 16)
     def _(i):
-        rows = pl.ds(pl.multiple_of(i * 16, 16), 16)
-        x = x_ref[rows, :].astype(F32)
-        inv = lax.rsqrt(jnp.mean(x * x, axis=-1, keepdims=True) + EPSILON)
-        xn_buf[rows, :] = (x * inv * gain).astype(BF16)
+        for j in range(16):
+            r = i * 16 + j
+            cos_ref[pl.ds(r, 1), :] = len_ref[r].astype(F32) * freq_ref[...]
+
+    @pl.loop(0, ROWS // 64)
+    def _(i):
+        rows = pl.ds(pl.multiple_of(i * 64, 64), 64)
+        angles = cos_ref[rows, :]
+        cos_ref[rows, :] = jnp.cos(angles)
+        sin_ref[rows, :] = jnp.sin(angles)
+
+    gain = 1.0 + wn_ref[...].astype(F32).reshape(1, D)
+
+    @pl.loop(0, ROWS // X_ROWS)
+    def _(n):
+        x_copy(n).wait()
+
+        @pl.loop(0, X_ROWS // 16)
+        def _(i):
+            rows = pl.ds(pl.multiple_of(n * X_ROWS + i * 16, 16), 16)
+            x = xn_buf[rows, :].astype(F32)
+            inv = lax.rsqrt(jnp.mean(x * x, axis=-1, keepdims=True) + EPSILON)
+            xn_buf[rows, :] = (x * inv * gain).astype(BF16)
 
     def rotate(u, rows):
         u = u.astype(BF16).astype(F32)
@@ -141,33 +172,48 @@
         for copy in cache_copies(g):
             copy.wait()
         chunk = g // G_PER_CHUNK
-        m_tile = stat_buf[chunk, 0]
-        d_tile = stat_buf[chunk, 1]
-        for pair in range(GROUP // 2):
-            r0 = g * GROUP + 2 * pair
-            lims = [len_ref[r0 + a] - base for a in range(2)]
-            keys = jnp.concatenate([patched(k_buf, slot, 2 * pair + a, knew_ref[pl.ds(r0 + a, 1), :], lims[a]) for a in range(2)], axis=0)
-            q_rows = pl.ds(pl.multiple_of(r0 * HEADS, 16), 16)
-            q2 = jnp.concatenate([q_buf[0, q_rows, :], q_buf[1, q_rows, :]], axis=1).astype(BF16)
-            s2 = lax.dot_general(q2, keys, (((1,), (1,)), ((), ())), preferred_element_type=F32)
-            probs = []
-            for a in range(2):
-                s = s2[a * HEADS:(a + 1) * HEADS, a * SLOTS:(a + 1) * SLOTS]
-                valid = lane <= lims[a]
-                m = jnp.max(jnp.where(valid, s, LOWEST), axis=-1, keepdims=True)
-                p = jnp.where(valid, jnp.exp(s - m), 0.0)
-                den = jnp.sum(p, axis=-1, keepdims=True)
-                here = lane == (g % G_PER_CHUNK) * GROUP + 2 * pair + a
-                m_tile = jnp.where(here, m, m_tile)
-                d_tile = jnp.where(here, den, d_tile)
-                probs.append(p)
-            zero = jnp.zeros((HEADS, SLOTS), F32)
-            p2 = jnp.concatenate([jnp.concatenate([probs[0], zero], axis=1), jnp.concatenate([zero, probs[1]], axis=1)], axis=0).astype(BF16)
-            values = jnp.concatenate([patched(v_buf, slot, 2 * pair + a, vnew_ref[pl.ds(r0 + a, 1), :], lims[a]) for a in range(2)], axis=0)
-            num_buf[pl.ds(pl.multiple_of(r0 * HEADS, 16), 16), :] = dot(p2, values)
-        stat_buf[chunk, 0] = m_tile
-        stat_buf[chunk, 1] = d_tile
-
+
+        UN = 8
+        @pl.loop(0, GROUP // 2 // UN)
+        def _(u):
+            m_tile = stat_buf[chunk, 0]
+            d_tile = stat_buf[chunk, 1]
+            for pp in range(UN):
+                pair = u * UN + pp
+                r0 = g * GROUP + 2 * pair
+                lims = [len_ref[r0 + a] - base for a in range(2)]
+                keys = jnp.concatenate([patched(k_buf, slot, 2 * pair + a, knew_ref[pl.ds(r0 + a, 1), :], lims[a]) for a in range(2)], axis=0)
+                q_rows = pl.ds(pl.multiple_of(r0 * HEADS, 16), 16)
+                q2 = jnp.concatenate([q_buf[0, q_rows, :], q_buf[1, q_rows, :]], axis=1).astype(BF16)
+                s2 = lax.dot_general(q2, keys, (((1,), (1,)), ((), ())), preferred_element_type=F32)
+                probs = []
+                for a in range(2):
+                    s = s2[a * HEADS:(a + 1) * HEADS, a * SLOTS:(a + 1) * SLOTS]
+                    valid = lane <= lims[a]
+                    m = jnp.max(jnp.where(valid, s, LOWEST), axis=-1, keepdims=True)
+                    p = jnp.where(valid, jnp.exp(s - m), 0.0)
+                    den = jnp.sum(p, axis=-1, keepdims=True)
+                    here = lane == (g % G_PER_CHUNK) * GROUP + 2 * pair + a
+                    m_tile = jnp.where(here, m, m_tile)
+                    d_tile = jnp.where(here, den, d_tile)
+                    probs.append(p)
+                zero = jnp.zeros((HEADS, SLOTS), F32)
+                p2 = jnp.concatenate([jnp.concatenate([probs[0], zero], axis=1), jnp.concatenate([zero, probs[1]], axis=1)], axis=0).astype(BF16)
+                p_buf[pair] = p2
+            stat_buf[chunk, 0] = m_tile
+            stat_buf[chunk, 1] = d_tile
+
+        @pl.loop(0, GROUP // 2 // UN)
+        def _(u):
+            for pp in range(UN):
+                pair = u * UN + pp
+                r0 = g * GROUP + 2 * pair
+                lims = [len_ref[r0 + a] - base for a in range(2)]
+                values = jnp.concatenate([patched(v_buf, slot, 2 * pair + a, vnew_ref[pl.ds(r0 + a, 1), :], lims[a]) for a in range(2)], axis=0)
+                o2 = dot(p_buf[pair], values)
+                q_rows = pl.ds(pl.multiple_of(r0 * HEADS, 16), 16)
+                q_buf[0, q_rows, :] = o2[:, :half]
+                q_buf[1, q_rows, :] = o2[:, half:]
         @pl.when(g + RING < N_GROUPS)
         def _():
             for copy in cache_copies(g + RING):
@@ -187,7 +233,7 @@
             (f_recv, f_stat, first_peer, my_half + (1 - first_bit) * quarter_rows, quarter_rows),
             (s_recv, s_stat, second_peer, my_quarter + (1 - second_bit) * EIGHTH, EIGHTH))[stage]
         return (pltpu.make_async_remote_copy(
-                    src_ref=num_buf.at[num_rows(k, offset, count), :], dst_ref=recv.at[k],
+                    src_ref=q_buf.at[:, num_rows(k, offset, count), :], dst_ref=recv.at[k],
                     send_sem=send_sem.at[stage, k], recv_sem=recv_sem.at[stage, k],
                     device_id={'sp': peer}, device_id_type=MESH_ID),
                 pltpu.make_async_remote_copy(
@@ -219,12 +265,9 @@
         start = (k * CHUNK + offset) * HEADS
         for r in range(count):
             dst = pl.ds(pl.multiple_of(start + r * HEADS, HEADS), HEADS)
-            total = num_buf[dst, :] * f_a[:, r:r + 1] + recv[k, r * HEADS:(r + 1) * HEADS, :] * f_b[:, r:r + 1]
-            if last:
-                att_buf[0, r * HEADS:(r + 1) * HEADS, :] = total[:, :half]
-                att_buf[1, r * HEADS:(r + 1) * HEADS, :] = total[:, half:]
-            else:
-                num_buf[dst, :] = total
+            a, b = f_a[:, r:r + 1], f_b[:, r:r + 1]
+            for i in range(2):
+                q_buf[i, dst, :] = q_buf[i, dst, :] * a + recv[k, i, r * HEADS:(r + 1) * HEADS, :] * b
 
     def send(stage, k):
         for copy in exchange(stage, k):
@@ -233,16 +276,16 @@
     def project_out(k):
         atts = []
         for h in range(HEADS):
-            heads = pl.ds(h, EIGHTH, stride=HEADS)
-            atts.append(jnp.concatenate([att_buf[0, heads, :], att_buf[1, heads, :]], axis=1).astype(BF16))
-        x_rows = pl.ds(pl.multiple_of(k * CHUNK + my_eighth, EIGHTH), EIGHTH)
+            heads = pl.ds((k * CHUNK + my_eighth) * HEADS + h, EIGHTH, stride=HEADS)
+            atts.append(jnp.concatenate([q_buf[0, heads, :], q_buf[1, heads, :]], axis=1).astype(BF16))
+        own_copy(k).wait()
         o_rows = pl.ds(pl.multiple_of(k * EIGHTH, EIGHTH), EIGHTH)
         for n in range(D // 512):
             cols = slice(n * 512, (n + 1) * 512)
             acc = dot(atts[0], w_buf[0:HEAD, cols])
             for h in range(1, HEADS):
                 acc += dot(atts[h], w_buf[h * HEAD:(h + 1) * HEAD, cols])
-            out_ref[o_rows, cols] = (x_ref[x_rows, cols].astype(F32) + acc).astype(BF16).astype(F32)
+            out_ref[o_rows, cols] = (x_own[k, :, cols].astype(F32) + acc).astype(BF16).astype(F32)
 
     @pl.loop(0, N_CHUNKS + 3)
     def _(t):
@@ -285,40 +328,44 @@
                 copy.wait_send()
 
 
-def attend(hidden, w_norm, cos_t, sin_t, cache_len, w_q, w_k, w_v, w_o, k_block, v_block):
+def attend(cache_len, inv_freq, w_norm, hidden, w_q, w_k, w_v, w_o, k_block, v_block):
     vmem = pl.BlockSpec(memory_space=pltpu.VMEM)
     hbm = pl.BlockSpec(memory_space=pl.ANY)
     return pl.pallas_call(
         attend_kernel,
-        out_shape=(jax.ShapeDtypeStruct((ROWS // 8, D), F32), jax.ShapeDtypeStruct((ROWS, HEAD), F32), jax.ShapeDtypeStruct((ROWS, HEAD), F32)),
-        in_specs=[vmem, vmem, vmem, vmem, pl.BlockSpec(memory_space=pltpu.SMEM)] + [hbm] * 6,
-        out_specs=(vmem, vmem, vmem),
+        out_shape=(pltpu.VMEM((ROWS // 8, D), F32), pltpu.VMEM((ROWS, HEAD), F32), pltpu.VMEM((ROWS, HEAD), F32),
+                   pltpu.VMEM((RING, GROUP, SLOTS, HEAD), BF16), pltpu.VMEM((RING, GROUP, SLOTS, HEAD), BF16)),
+        in_specs=[pl.BlockSpec(memory_space=pltpu.SMEM), vmem, vmem] + [hbm] * 7,
+        out_specs=(vmem,) * 5,
         scratch_shapes=[
             pltpu.VMEM((D, D), BF16), pltpu.VMEM((2, D, HEAD), BF16), pltpu.VMEM((ROWS, D), BF16),
-            pltpu.VMEM((2, ROWS * HEADS, HEAD // 2), F32),
-            pltpu.VMEM((RING, GROUP, SLOTS, HEAD), BF16), pltpu.VMEM((RING, GROUP, SLOTS, HEAD), BF16),
-            pltpu.VMEM((ROWS * HEADS, HEAD), F32), pltpu.VMEM((3 * N_CHUNKS, 2, HEADS, CHUNK), F32),
-            pltpu.VMEM((N_CHUNKS, CHUNK // 2 * HEADS, HEAD), F32),
-            pltpu.VMEM((N_CHUNKS, CHUNK // 4 * HEADS, HEAD), F32),
-            pltpu.VMEM((N_CHUNKS, EIGHTH * HEADS, HEAD), F32),
+            pltpu.VMEM((N_CHUNKS, EIGHTH, D), BF16),
+            pltpu.VMEM((ROWS, HEAD // 2), F32), pltpu.VMEM((ROWS, HEAD // 2), F32),
+            pltpu.VMEM((2, ROWS * HEADS, HEAD // 2), F32), pltpu.VMEM((3 * N_CHUNKS, 2, HEADS, CHUNK), F32),
+            pltpu.VMEM((N_CHUNKS, 2, CHUNK // 2 * HEADS, HEAD // 2), F32),
+            pltpu.VMEM((N_CHUNKS, 2, CHUNK // 4 * HEADS, HEAD // 2), F32),
+            pltpu.VMEM((N_CHUNKS, 2, EIGHTH * HEADS, HEAD // 2), F32),
             pltpu.VMEM((N_CHUNKS, 2, HEADS, CHUNK), F32), pltpu.VMEM((N_CHUNKS, 2, HEADS, CHUNK), F32), pltpu.VMEM((N_CHUNKS, 2, HEADS, CHUNK), F32),
-            pltpu.VMEM((2, EIGHTH * HEADS, HEAD // 2), F32),
+            pltpu.VMEM((GROUP // 2, 16, 2 * SLOTS), BF16),
+            pltpu.SemaphoreType.DMA((ROWS // X_ROWS,)), pltpu.SemaphoreType.DMA((N_CHUNKS,)),
             pltpu.SemaphoreType.DMA((HEADS,)), pltpu.SemaphoreType.DMA((2,)),
             pltpu.SemaphoreType.DMA((RING,)), pltpu.SemaphoreType.DMA((RING,)),
             pltpu.SemaphoreType.DMA((3, N_CHUNKS)), pltpu.SemaphoreType.DMA((3, N_CHUNKS)),
             pltpu.SemaphoreType.DMA((3, N_CHUNKS)), pltpu.SemaphoreType.DMA((3, N_CHUNKS)),
         ],
-        compiler_params=pltpu.CompilerParams(collective_id=0, has_side_effects=True, vmem_limit_bytes=60 * 2 ** 20),
+        compiler_params=pltpu.CompilerParams(collective_id=0, has_side_effects=True, vmem_limit_bytes=24 * 2 ** 20),
         cost_estimate=pl.CostEstimate(flops=20 * 10 ** 9, bytes_accessed=90 * 10 ** 6, transcendentals=0),
-    )(hidden, w_norm, cos_t, sin_t, cache_len, w_q, w_k, w_v, w_o, k_block, v_block)
+    )(cache_len, inv_freq, w_norm, hidden, w_q, w_k, w_v, w_o, k_block, v_block)
 
 
 COPY_RING = 8
-
-
-def cache_kernel(len_ref, knew_ref, vnew_ref, k_hbm, v_hbm, ko_hbm, vo_hbm, buf, in_sem, out_sem):
+N_STREAM = N_GROUPS - RING
+
+
+def cache_kernel(len_ref, knew_ref, vnew_ref, k_held, v_held, k_hbm, v_hbm, ko_hbm, vo_hbm, buf, in_sem, out_sem, held_sem):
     base = lax.axis_index('sp') * SLOTS
     sub16 = lax.broadcasted_iota(jnp.int32, (16, HEAD), 0)
+    held = (k_held, v_held)
 
     def ins(g):
         slot, rows = g % COPY_RING, pl.ds(g * GROUP, GROUP)
@@ -327,15 +374,35 @@
     def outs(g):
         slot, rows = g % COPY_RING, pl.ds(g * GROUP, GROUP)
         return [pltpu.make_async_copy(buf.at[i, slot], dst.at[rows], out_sem.at[i, slot]) for i, dst in enumerate((ko_hbm, vo_hbm))]
+
+    def held_outs(h):
+        rows = pl.ds((N_STREAM + h) * GROUP, GROUP)
+        return [pltpu.make_async_copy(held[i].at[(N_STREAM + h) % RING], dst.at[rows], held_sem.at[i, h]) for i, dst in enumerate((ko_hbm, vo_hbm))]
+
+    def patch(g, i, ref, index):
+        new_ref = (knew_ref, vnew_ref)[i]
+        for j in range(GROUP):
+            r = g * GROUP + j
+            at = len_ref[r] - base
+            tile = jnp.clip(at, 0, SLOTS - 1) // 16 * 16
+            span = pl.ds(pl.multiple_of(tile, 16), 16)
+            new = jnp.broadcast_to(new_ref[pl.ds(r, 1), :], (16, HEAD))
+            where = (*index, j, span, slice(None))
+            ref[where] = jnp.where(sub16 == at - tile, new, ref[where].astype(F32)).astype(BF16)
 
     ahead = COPY_RING // 2
     for g in range(ahead):
         for copy in ins(g):
             copy.start()
 
-    @pl.loop(0, N_GROUPS)
+    @pl.loop(0, N_STREAM)
     def _(g):
-        @pl.when(g + ahead < N_GROUPS)
+        for i in range(2):
+            patch(N_STREAM + g, i, held[i], ((N_STREAM + g) % RING,))
+        for copy in held_outs(g):
+            copy.start()
+
+        @pl.when(g + ahead < N_STREAM)
         def _():
             @pl.when(g + ahead >= COPY_RING)
             def _():
@@ -345,39 +412,37 @@
                 copy.start()
         for copy in ins(g):
             copy.wait()
-        slot = g % COPY_RING
-        for j in range(GROUP):
-            r = g * GROUP + j
-            at = len_ref[r] - base
-            tile = jnp.clip(at, 0, SLOTS - 1) // 16 * 16
-            span = pl.ds(pl.multiple_of(tile, 16), 16)
-            hit = sub16 == at - tile
-            for i, new_ref in enumerate((knew_ref, vnew_ref)):
-                new = jnp.broadcast_to(new_ref[pl.ds(r, 1), :], (16, HEAD))
-                old = buf[i, slot, j, span, :].astype(F32)
-                buf[i, slot, j, span, :] = jnp.where(hit, new, old).astype(BF16)
+        for i in range(2):
+            patch(g, i, buf, (i, g % COPY_RING))
         for copy in outs(g):
             copy.start()
 
-    @pl.loop(N_GROUPS - COPY_RING, N_GROUPS)
+    @pl.loop(N_STREAM - COPY_RING, N_STREAM)
     def _(g):
         for copy in outs(g):
             copy.wait()
 
-
-def update_caches(cache_len, k_new, v_new, k_block, v_block):
+    @pl.loop(0, RING)
+    def _(h):
+        for copy in held_outs(h):
+            copy.wait()
+
+
+def update_caches(cache_len, k_new, v_new, k_held, v_held, k_block, v_block):
     vmem = pl.BlockSpec(memory_space=pltpu.VMEM)
     hbm = pl.BlockSpec(memory_space=pl.ANY)
     shape = jax.ShapeDtypeStruct(k_block.shape, k_block.dtype)
+    k_new, v_new, k_held, v_held = [pltpu.with_memory_space_constraint(a, pltpu.VMEM) for a in (k_new, v_new, k_held, v_held)]
     return pl.pallas_call(
         cache_kernel,
         out_shape=(shape, shape),
-        in_specs=[pl.BlockSpec(memory_space=pltpu.SMEM), vmem, vmem, hbm, hbm],
+        in_specs=[pl.BlockSpec(memory_space=pltpu.SMEM), vmem, vmem, vmem, vmem, hbm, hbm],
         out_specs=(hbm, hbm),
-        scratch_shapes=[pltpu.VMEM((2, COPY_RING, GROUP, SLOTS, HEAD), BF16), pltpu.SemaphoreType.DMA((2, COPY_RING)), pltpu.SemaphoreType.DMA((2, COPY_RING))],
-        compiler_params=pltpu.CompilerParams(vmem_limit_bytes=40 * 2 ** 20),
+        scratch_shapes=[pltpu.VMEM((2, COPY_RING, GROUP, SLOTS, HEAD), BF16), pltpu.SemaphoreType.DMA((2, COPY_RING)), pltpu.SemaphoreType.DMA((2, COPY_RING)),
+                        pltpu.SemaphoreType.DMA((2, RING))],
+        compiler_params=pltpu.CompilerParams(vmem_limit_bytes=24 * 2 ** 20),
         cost_estimate=pl.CostEstimate(flops=20 * 10 ** 9, bytes_accessed=134 * 10 ** 6, transcendentals=0),
-    )(cache_len, k_new, v_new, k_block, v_block)
+    )(cache_len, k_new, v_new, k_held, v_held, k_block, v_block)
 
 
 PIECES = (0, 2, 4, 6, 1, 3, 5, 7)
@@ -407,15 +472,15 @@
 
 
 def local_step(hidden, w_norm, w_q, w_k, w_v, w_o, k_block, v_block, cache_len):
-    inv_freq = ROPE_BASE ** (-jnp.arange(HEAD // 2, dtype=F32) * 2.0 / HEAD)
-    angles = cache_len.astype(F32)[:, None] * inv_freq[None, :]
-    own, k_new, v_new = attend(hidden, w_norm[None, :], jnp.cos(angles), jnp.sin(angles), cache_len, w_q, w_k, w_v, w_o, k_block, v_block)
+    inv_freq = np.float32(ROPE_BASE) ** (-np.arange(HEAD // 2, dtype=np.float32) * np.float32(2.0 / HEAD))
+    own, k_new, v_new, k_held, v_held = attend(cache_len, inv_freq[None, :], w_norm, hidden, w_q, w_k, w_v, w_o, k_block, v_block)
 
     def flip(array, bits):
         return lax.ppermute(array, 'sp', [(i, i ^ bits) for i in range(8)])
 
     held = [own] + [flip(own, bits) for bits in (2, 4, 6)]
-    new_k, new_v = update_caches(cache_len, k_new, v_new, k_block, v_block)
+    new_k, new_v = update_caches(cache_len, k_new, v_new, k_held, v_held, k_block, v_block)
+    *held, new_k = lax.optimization_barrier((*held, new_k))
     other = [flip(piece, 1) for piece in held]
     return assemble(held + other), new_k, new_v
 

time: 192 us -> 121 us (0.63)
  Pallas kernels: 159 us -> 101 us
  waiting for transfers between devices: 21.7 us -> 2.39 us
  local copies, waits for them, and re-layouts: 4.5 us -> 12.7 us
  other arithmetic: 2.49 us -> 0 us
    pallas_call x1, Pallas kernels: 109 us -> 63 us  [attend(): pl.pallas_call(attend_kernel, out_shape=(pltpu.VMEM((ROWS // 8, D), F32),...]
    ppermute x7, waiting for transfers between devices: 21.7 us -> 2.39 us  [flip(): return lax.ppermute(array, 'sp', [(i, i ^ bits) for i in range(8)])]
    pallas_call x1, Pallas kernels: 45.2 us -> 33.1 us  [update_caches(): pl.pallas_call(cache_kernel, out_shape=(shape, shape), in_specs=[pl.Block...]
    unnamed x18, local copies, waits for them, and re-layouts: 3.21 us -> 12.7 us
  transfers between devices with their start and end apart: 7 -> 7, of which waited for: 3 -> 3; matrix products, arithmetic and copies ran while one was open for 0% -> 0% of each run, Pallas kernels for 24% -> 27%
where the time goes in v2:
time: 121 us
  Pallas kernels  101 us (83%)
  local copies, waits for them, and re-layouts  12.7 us (10%)
  starting transfers between devices  4.63 us (4%)
  waiting for transfers between devices  2.39 us (2%)
    pallas_call x1, Pallas kernels, attend(): pl.pallas_call(attend_kernel, out_shape=(pltpu.VMEM((ROWS // 8, D), F32),...  63 us
    pallas_call x1, Pallas kernels, update_caches(): pl.pallas_call(cache_kernel, out_shape=(shape, shape), in_specs=[pl.Block...  33.1 us
    unnamed x18, local copies, waits for them, and re-layouts  12.7 us
    ppermute x7, starting transfers between devices, flip(): return lax.ppermute(array, 'sp', [(i, i ^ bits) for i in range(8)])  4.63 us
    pallas_call x1, Pallas kernels, assemble(): pl.pallas_call(assemble_kernel, grid=(N_CHUNKS,), out_shape=jax.ShapeDtyp...  4.56 us
  transfers between devices with their start and end apart: 7, of which 3 were waited for; matrix products, arithmetic and copies ran while one was open for 0% of the time, Pallas kernels for 27%

profile of v2, /device:TPU:0, one launch (start us, length us, event | category | flops | bytes accessed | tf_op | source)
XLA Modules:
  0.0 121.2 jit_solution(792049939047773163)
XLA Ops:
  0.6 63.0 %shard_map.121 = (f32[64,2048]{1,0:T(8,128)S(1)}, f32[512,256]{1,0:T(8,128)S(1)}, f32[512,256]{1,0:T(8,128)S(1)}, bf16[16,16,128,256]{3,2,1,0:T(8,128)(2,1)S(1)}, bf16[16,16,128,256]{3,2,1,0:T(8,128)(2,1)S(1)}) custom-call(s32[512]{0:T(512)} %len_ref.3, f32[1,128]{1,0:T(1,128)} %constant.2.clone.freq_ref, bf16[2048]{0:T(1024)(128)(2,1)} %wn_ref.1, ...), custom_call_target="tpu_custom_call" | custom-call | flops 20000000000 | bytes 90000000 | tf_op jit(solution)/shard_map/pallas_call | solution.py:334
  63.6 0.0 copy-start
  63.6 6.2 %copy-done = bf16[16,16,128,256]{3,2,1,0:T(8,128)(2,1)} copy-done((bf16[16,16,128,256]{3,2,1,0:T(8,128)(2,1)}, bf16[16,16,128,256]{3,2,1,0:T(8,128)(2,1)S(1)}, u32[]{:S(2)}) %copy-start) | copy-done | bytes 16777240
  69.8 0.0 copy-start.2
  69.8 2.1 %collective-permute-start = (f32[64,2048]{1,0:T(8,128)S(1)}, f32[64,2048]{1,0:T(8,128)S(1)}, u32[]{:S(2)}, u32[]{:S(2)}) collective-permute-start(f32[64,2048]{1,0:T(8,128)S(1)} %get-tuple-element.21.refs_0_), channel_id=1, source_target_pairs={{0,2},{1,3},{2,0},{3,1},{4,6},{5,7},{6,4},{7,5}} | collective-permute-start | bytes 1572872 | tf_op jit(solution)/shard_map/ppermute | solution.py:479
  71.9 0.1 collective-permute-start.1
  72.0 1.4 %collective-permute-start.2 = (f32[64,2048]{1,0:T(8,128)S(1)}, f32[64,2048]{1,0:T(8,128)S(1)}, u32[]{:S(2)}, u32[]{:S(2)}) collective-permute-start(f32[64,2048]{1,0:T(8,128)S(1)} %get-tuple-element.21.refs_0_), channel_id=1, source_target_pairs={{0,6},{1,7},{2,4},{3,5},{4,2},{5,3},{6,0},{7,1}} | collective-permute-start | bytes 1572872 | tf_op jit(solution)/shard_map/ppermute | solution.py:479
  73.4 0.0 copy-start.1
  73.4 5.8 %copy-done.1 = bf16[16,16,128,256]{3,2,1,0:T(8,128)(2,1)S(1)} copy-done((bf16[16,16,128,256]{3,2,1,0:T(8,128)(2,1)S(1)}, bf16[16,16,128,256]{3,2,1,0:T(8,128)(2,1)}, u32[]{:S(2)}) %copy-start.1) | copy-done | bytes 16777240
  79.1 33.1 %shard_map.122 = (bf16[512,128,256]{2,1,0:T(8,128)(2,1)}, bf16[512,128,256]{2,1,0:T(8,128)(2,1)}) custom-call(s32[512]{0:T(512)} %len_ref.3, f32[512,256]{1,0:T(8,128)S(1)} %get-tuple-element.16.knew_ref, f32[512,256]{1,0:T(8,128)S(1)} %get-tuple-element.17.vnew_ref, bf16[16,16,128,256]{3,2,1,0:T(8,128)(2,1)S(1)} %copy-done.1, ...), custom_call_target="tpu_custom_call" | custom-call | flops 20000000000 | bytes 134000000 | tf_op jit(solution)/shard_map/pallas_call | solution.py:436
  112.3 0.0 collective-permute-done.refs_1_
  112.3 0.0 copy-start.3
  112.3 0.0 collective-permute-done.1.refs_2_
  112.3 0.0 copy-start.4
  112.3 0.0 collective-permute-done.2.refs_3_
  112.3 0.0 copy-start.5
  112.3 0.0 copy-done.2
  112.3 0.0 collective-permute-start.3
  112.4 0.5 collective-permute-start.4
  112.9 0.0 collective-permute-start.5
  112.9 0.5 collective-permute-start.6
  113.4 0.9 collective-permute-done.3.refs_4_
  114.3 0.0 copy-start.6
  114.3 0.7 collective-permute-done.4.refs_5_
  115.0 0.0 copy-start.7
  115.0 0.7 collective-permute-done.5.refs_6_
  115.8 0.0 copy-start.8
  115.8 0.8 copy-done.8
  116.6 0.0 collective-permute-done.6.refs_7_
  116.6 0.0 copy-done.3
  116.6 0.0 copy-done.4
  116.6 0.0 copy-done.5
  116.6 0.0 copy-done.6
  116.6 0.0 copy-done.7
  116.6 4.6 %shard_map.123 = bf16[512,2048]{1,0:T(8,128)(2,1)} custom-call(f32[64,2048]{1,0:T(8,128)} %copy-done.2, f32[64,2048]{1,0:T(8,128)} %copy-done.3, f32[64,2048]{1,0:T(8,128)} %copy-done.4, f32[64,2048]{1,0:T(8,128)} %copy-done.5, f32[64,2048]{1,0:T(8,128)} %copy-done.6, f32[64,2048]{1,0:T(8,128)} %copy-done.7, f32[64,2048]{1,0:T(8,128)} %copy-done.8, ...), custom_call_target="tpu_custom_call" | custom-call | flops 1000000000 | bytes 6291456 | tf_op jit(solution)/shard_map/pallas_call | solution.py:464
Async XLA Ops:
  63.6 6.2 %copy-start = (bf16[16,16,128,256]{3,2,1,0:T(8,128)(2,1)}, bf16[16,16,128,256]{3,2,1,0:T(8,128)(2,1)S(1)}, u32[]{:S(2)}) copy-start(bf16[16,16,128,256]{3,2,1,0:T(8,128)(2,1)S(1)} %get-tuple-element.18.k_held) | copy-start | bytes 50331652
  69.8 42.6 %copy-start.2 = (f32[64,2048]{1,0:T(8,128)}, f32[64,2048]{1,0:T(8,128)S(1)}, u32[]{:S(2)}) copy-start(f32[64,2048]{1,0:T(8,128)S(1)} %get-tuple-element.21.refs_0_) | copy-start | bytes 1572868
  69.8 42.5 %collective-permute-start = (f32[64,2048]{1,0:T(8,128)S(1)}, f32[64,2048]{1,0:T(8,128)S(1)}, u32[]{:S(2)}, u32[]{:S(2)}) collective-permute-start(f32[64,2048]{1,0:T(8,128)S(1)} %get-tuple-element.21.refs_0_), channel_id=1, source_target_pairs={{0,2},{1,3},{2,0},{3,1},{4,6},{5,7},{6,4},{7,5}} | collective-permute-start | bytes 1572872 | tf_op jit(solution)/shard_map/ppermute | solution.py:479
  71.9 40.4 %collective-permute-start.1 = (f32[64,2048]{1,0:T(8,128)S(1)}, f32[64,2048]{1,0:T(8,128)S(1)}, u32[]{:S(2)}, u32[]{:S(2)}) collective-permute-start(f32[64,2048]{1,0:T(8,128)S(1)} %get-tuple-element.21.refs_0_), channel_id=1, source_target_pairs={{0,4},{1,5},{2,6},{3,7},{4,0},{5,1},{6,2},{7,3}} | collective-permute-start | bytes 1572872 | tf_op jit(solution)/shard_map/ppermute | solution.py:479
  72.0 40.4 %collective-permute-start.2 = (f32[64,2048]{1,0:T(8,128)S(1)}, f32[64,2048]{1,0:T(8,128)S(1)}, u32[]{:S(2)}, u32[]{:S(2)}) collective-permute-start(f32[64,2048]{1,0:T(8,128)S(1)} %get-tuple-element.21.refs_0_), channel_id=1, source_target_pairs={{0,6},{1,7},{2,4},{3,5},{4,2},{5,3},{6,0},{7,1}} | collective-permute-start | bytes 1572872 | tf_op jit(solution)/shard_map/ppermute | solution.py:479
  73.4 5.8 %copy-start.1 = (bf16[16,16,128,256]{3,2,1,0:T(8,128)(2,1)S(1)}, bf16[16,16,128,256]{3,2,1,0:T(8,128)(2,1)}, u32[]{:S(2)}) copy-start(bf16[16,16,128,256]{3,2,1,0:T(8,128)(2,1)} %copy-done) | copy-start | bytes 50331652
  112.3 4.3 %copy-start.3 = (f32[64,2048]{1,0:T(8,128)}, f32[64,2048]{1,0:T(8,128)S(1)}, u32[]{:S(2)}) copy-start(f32[64,2048]{1,0:T(8,128)S(1)} %collective-permute-done.refs_1_) | copy-start | bytes 1572868
  112.3 4.3 %copy-start.4 = (f32[64,2048]{1,0:T(8,128)}, f32[64,2048]{1,0:T(8,128)S(1)}, u32[]{:S(2)}) copy-start(f32[64,2048]{1,0:T(8,128)S(1)} %collective-permute-done.1.refs_2_) | copy-start | bytes 1572868
  112.3 4.3 %copy-start.5 = (f32[64,2048]{1,0:T(8,128)}, f32[64,2048]{1,0:T(8,128)S(1)}, u32[]{:S(2)}) copy-start(f32[64,2048]{1,0:T(8,128)S(1)} %collective-permute-done.2.refs_3_) | copy-start | bytes 1572868
  112.3 1.9 %collective-permute-start.3 = (f32[64,2048]{1,0:T(8,128)S(1)}, f32[64,2048]{1,0:T(8,128)S(1)}, u32[]{:S(2)}, u32[]{:S(2)}) collective-permute-start(f32[64,2048]{1,0:T(8,128)S(1)} %get-tuple-element.21.refs_0_), channel_id=1, source_target_pairs={{0,1},{1,0},{2,3},{3,2},{4,5},{5,4},{6,7},{7,6}} | collective-permute-start | bytes 1572872 | tf_op jit(solution)/shard_map/ppermute | solution.py:479
  112.4 2.6 %collective-permute-start.4 = (f32[64,2048]{1,0:T(8,128)S(1)}, f32[64,2048]{1,0:T(8,128)S(1)}, u32[]{:S(2)}, u32[]{:S(2)}) collective-permute-start(f32[64,2048]{1,0:T(8,128)S(1)} %collective-permute-done.refs_1_), channel_id=1, source_target_pairs={{0,1},{1,0},{2,3},{3,2},{4,5},{5,4},{6,7},{7,6}} | collective-permute-start | bytes 1572872 | tf_op jit(solution)/shard_map/ppermute | solution.py:479
  112.9 2.9 %collective-permute-start.5 = (f32[64,2048]{1,0:T(8,128)S(1)}, f32[64,2048]{1,0:T(8,128)S(1)}, u32[]{:S(2)}, u32[]{:S(2)}) collective-permute-start(f32[64,2048]{1,0:T(8,128)S(1)} %collective-permute-done.1.refs_2_), channel_id=1, source_target_pairs={{0,1},{1,0},{2,3},{3,2},{4,5},{5,4},{6,7},{7,6}} | collective-permute-start | bytes 1572872 | tf_op jit(solution)/shard_map/ppermute | solution.py:479
  112.9 3.7 %collective-permute-start.6 = (f32[64,2048]{1,0:T(8,128)S(1)}, f32[64,2048]{1,0:T(8,128)}, u32[]{:S(2)}, u32[]{:S(2)}) collective-permute-start(f32[64,2048]{1,0:T(8,128)S(1)} %collective-permute-done.2.refs_3_), channel_id=1, source_target_pairs={{0,1},{1,0},{2,3},{3,2},{4,5},{5,4},{6,7},{7,6}} | collective-permute-start | bytes 1572872 | tf_op jit(solution)/shard_map/ppermute | solution.py:479
  114.3 2.3 %copy-start.6 = (f32[64,2048]{1,0:T(8,128)}, f32[64,2048]{1,0:T(8,128)S(1)}, u32[]{:S(2)}) copy-start(f32[64,2048]{1,0:T(8,128)S(1)} %collective-permute-done.3.refs_4_) | copy-start | bytes 1572868
  115.0 1.6 %copy-start.7 = (f32[64,2048]{1,0:T(8,128)}, f32[64,2048]{1,0:T(8,128)S(1)}, u32[]{:S(2)}) copy-start(f32[64,2048]{1,0:T(8,128)S(1)} %collective-permute-done.4.refs_5_) | copy-start | bytes 1572868
  115.8 0.8 copy-start.8
